TPU v7x, 256 devices: a whole 4x4x8 slice. The times are simulated.
256 devices in a mesh: row: 32 (over y, z), col: 8 (over x, core).
Axes of the slice: x: 4, y: 4, z: 8, core: 2. Of those that a mesh axis runs over, the one named last changes fastest.
Arguments:
- sim_window: bfloat16 [6144, 6144], P('row', 'col'), as said below
- sim_rest: bfloat16 [6144, 113856], P('row', 'col'), may hold values from -6 to 6
- joined_partner_pairs: int32 [768, 2], replicated, may hold values from 0 to 6143, as said below
- cluster_member_count: int32 [6144], replicated, may hold values from 1 to 64
Outputs:
- window_out: bfloat16 [6144, 6144], P('row', 'col')
- rest_out: bfloat16 [6144, 113856], P('row', 'col')
Inputs may be any that keep to these rules, and one draw needn't show every extreme that they name: `joined_partner_pairs`: each row is (survivor, partner); no window item appears twice in the whole list. Each aligned block of 192 items holds exactly 24 partners. For any two aligned blocks (possibly the same), at most 3 pairs have their partner in the first and their survivor in the second, and some two blocks have exactly 3. Nearly symmetric: sim_window[i, j] is close to sim_window[j, i].
All inputs are finite; a program needn't handle non-finite values.
Results may differ from a plain program's by a relative error of at most 0.001.
Values may be sent and summed in bfloat16 or wider, within the bound.
No kernel may reach another device: no remote copies, remote signals or barrier semaphores. Data moves between devices by JAX's collectives and lax.ppermute only.
A program may use at most 128 MiB of HBM per device.

v0:
```python
import jax
import jax.numpy as jnp
from jax import lax
from jax.sharding import PartitionSpec as P


def pairing_tables(joined_partner_pairs, cluster_member_count):
    lasting_node = joined_partner_pairs[:, 0]
    vanishing_node = joined_partner_pairs[:, 1]
    remaining_size = cluster_member_count[lasting_node].astype(jnp.float32)
    absorbed_size = cluster_member_count[vanishing_node].astype(jnp.float32)
    joined_cluster_size = remaining_size + absorbed_size
    return (
        lasting_node,
        vanishing_node,
        remaining_size / joined_cluster_size,
        absorbed_size / joined_cluster_size,
    )


def item_weight_values(node_labels, lasting_node, vanishing_node, retained_pair, selected_pair):
    lasting_mask = node_labels[:, None] == lasting_node[None, :]
    belongs_mask = node_labels[:, None] == vanishing_node[None, :]
    lasting_real_mask = lasting_mask.astype(jnp.float32)
    matched_mask = jnp.sum((lasting_mask | belongs_mask).astype(jnp.float32), axis=1)
    retained_entries = (
        1.0 - matched_mask + jnp.sum(lasting_real_mask * retained_pair[None, :], axis=1)
    )
    selected_entries = jnp.sum(lasting_real_mask * selected_pair[None, :], axis=1)
    donor_position = jnp.sum(jnp.where(lasting_mask, vanishing_node[None, :], 0), axis=1)
    return (retained_entries, selected_entries, donor_position)


def shards(sim_window, sim_rest, joined_partner_pairs, cluster_member_count):
    row_number_total = sim_window.shape[0]
    col_count = sim_window.shape[1]
    blocks = lax.axis_size("row")
    local_block = lax.axis_index("row")
    my_col = lax.axis_index("col")
    lasting_node, vanishing_node, retained_pair, selected_pair = pairing_tables(
        joined_partner_pairs, cluster_member_count
    )
    row_sequence = jnp.arange(row_number_total, dtype=jnp.int32)
    retained_entries, selected_entries, ignored = item_weight_values(
        local_block * row_number_total + row_sequence,
        lasting_node,
        vanishing_node,
        retained_pair,
        selected_pair,
    )
    src_block = vanishing_node // row_number_total
    destination_block = lasting_node // row_number_total
    pair_count = joined_partner_pairs.shape[0]
    pair_order = jnp.arange(pair_count, dtype=jnp.int32)
    earlier = pair_order[None, :] < pair_order[:, None]
    slot_width = row_number_total // 8
    same_route = src_block[None, :] == src_block[:, None]
    slot_rank = jnp.sum((earlier & same_route).astype(jnp.int32), axis=1)
    recv_slot = src_block * slot_width + slot_rank
    recv_width = blocks * slot_width
    mine_src = src_block == local_block
    slot_hot = (
        (jnp.arange(slot_width, dtype=jnp.int32)[:, None] == slot_rank[None, :]) & mine_src[None, :]
    ).astype(jnp.bfloat16)
    row_hot = (
        (vanishing_node - local_block * row_number_total)[:, None] == row_sequence[None, :]
    ).astype(jnp.bfloat16)
    selector = jnp.dot(slot_hot, row_hot, preferred_element_type=jnp.float32).astype(jnp.bfloat16)
    send_window = jnp.dot(selector, sim_window, preferred_element_type=jnp.float32).astype(
        jnp.bfloat16
    )
    send_rest = jnp.dot(selector, sim_rest, preferred_element_type=jnp.float32).astype(jnp.bfloat16)
    local_destination = destination_block == local_block
    target_hot = (
        ((lasting_node - local_block * row_number_total)[None, :] == row_sequence[:, None])
        & local_destination[None, :]
    ).astype(jnp.bfloat16)
    recv_hot = (recv_slot[:, None] == jnp.arange(recv_width, dtype=jnp.int32)[None, :]).astype(
        jnp.bfloat16
    )
    placement = jnp.dot(target_hot, recv_hot, preferred_element_type=jnp.float32).astype(
        jnp.bfloat16
    )
    placed_window = jnp.dot(
        placement,
        lax.all_gather(send_window, "row", axis=0, tiled=True),
        preferred_element_type=jnp.float32,
    )
    placed_rest = jnp.dot(
        placement,
        lax.all_gather(send_rest, "row", axis=0, tiled=True),
        preferred_element_type=jnp.float32,
    )
    mixed_window = (
        retained_entries[:, None] * sim_window.astype(jnp.float32)
        + selected_entries[:, None] * placed_window
    ).astype(jnp.bfloat16)
    rest_out = (
        retained_entries[:, None] * sim_rest.astype(jnp.float32)
        + selected_entries[:, None] * placed_rest
    ).astype(jnp.bfloat16)
    col_iota = jnp.arange(col_count, dtype=jnp.int32)
    column_identifiers = my_col * col_count + col_iota
    column_retained, column_selected, column_provider = item_weight_values(
        column_identifiers, lasting_node, vanishing_node, retained_pair, selected_pair
    )
    piece = lax.all_gather(mixed_window, "col", axis=1, tiled=True)
    piece_width = piece.shape[1]
    picker = (jnp.arange(piece_width, dtype=jnp.int32)[:, None] == column_provider[None, :]).astype(
        jnp.bfloat16
    )
    gathered = jnp.dot(piece, picker, preferred_element_type=jnp.float32)
    window_out = (
        column_retained[None, :] * mixed_window.astype(jnp.float32)
        + column_selected[None, :] * gathered
    ).astype(jnp.bfloat16)
    return (window_out, rest_out)


def solution(mesh):
    in_specs = (P("row", "col"), P("row", "col"), P(), P())
    out_specs = (P("row", "col"), P("row", "col"))
    return jax.shard_map(shards, mesh=mesh, in_specs=in_specs, out_specs=out_specs, check_vma=False)
```

profile of v0, /device:TPU:1, one launch (start us, length us, event | category | flops | bytes accessed | tf_op | source)
XLA Modules:
  0.0 313.5 jit_solution(18282270828736118344)
XLA Ops:
  7.2 0.0 copy-start
  7.2 0.0 all-gather.4.cloned.1.call-start
  7.2 0.8 fusion.32
  8.1 0.4 convert_reduce_fusion
  8.5 0.3 convolution_convert_fusion.2
  8.7 1.8 convolution_convert_fusion.1
  10.5 0.0 all-gather.4.cloned.1.call-update
  10.6 0.0 all-gather.6.cloned.1.call-start
  10.6 4.5 %gather_fusion = s32[768]{0:T(1024)S(1)} fusion(s32[6144]{0:T(1024)S(1)} %copy-done, s32[1024]{0:T(1024)S(1)} %get-tuple-element.25), kind=kCustom, calls=%fused_computation | custom fusion | bytes 9216 | tf_op jit(solution)/shard_map/gather | solution.py:10
  15.1 4.5 %gather_fusion.1 = s32[768]{0:T(1024)S(1)} fusion(s32[6144]{0:T(1024)S(1)} %copy-done, s32[1024]{0:T(1024)S(1)} %get-tuple-element.24), kind=kCustom, calls=%fused_computation.1 | custom fusion | bytes 9216 | tf_op jit(solution)/shard_map/gather | solution.py:11
  19.6 0.3 convert_reduce_fusion.2
  20.0 0.8 fusion.14
  20.8 65.7 %all-gather.4.cloned.1.call-done = bf16[768,768]{1,0:T(8,128)(2,1)} async-done(((bf16[24,768]{1,0:T(8,128)(2,1)}), bf16[768,768]{1,0:T(8,128)(2,1)}) %all-gather.4.cloned.1.call-update) | async-done | bytes 1179664 | tf_op jit(solution)/shard_map/all_gather | solution.py:86
  86.5 2.4 fusion.13
  88.9 0.0 all-gather.6.cloned.1.call-update
  88.9 0.2 all-gather.8.cloned.1.call-start
  89.1 4.3 %convolution_convert_fusion = bf16[24,14232]{1,0:T(8,128)(2,1)} fusion(bf16[24,192]{1,0:T(8,128)(2,1)S(1)} %convolution_convert_fusion.2, bf16[192,14232]{1,0:T(8,128)(2,1)} %param.5), kind=kOutput, calls=%fused_computation.7 | convolution fusion | flops 131503680 | bytes 6157440 | tf_op jit(solution)/shard_map/dot_general | solution.py:72
  93.4 0.0 all-gather.8.cloned.1.call-update
  93.4 0.4 fusion.6
  93.8 0.9 convert_reduce_fusion.1
  94.7 25.4 %all-gather.6.cloned.1.call-done = bf16[192,6144]{1,0:T(8,128)(2,1)} async-done(((bf16[192,768]{1,0:T(8,128)(2,1)}), bf16[192,6144]{1,0:T(8,128)(2,1)}) %all-gather.6.cloned.1.call-update) | async-done | bytes 2359312 | tf_op jit(solution)/shard_map/all_gather | solution.py:107
  120.1 6.4 %fusion.12 = bf16[192,768]{1,0:T(8,128)(2,1)} fusion(bf16[192,6144]{1,0:T(8,128)(2,1)} %all-gather.6.cloned.1.call-done, s32[768]{0:T(1024)S(1)} %fusion.6, bf16[192,768]{1,0:T(8,128)(2,1)S(1)} %copy-done.1, f32[768]{0:T(1024)S(1)} %get-tuple-element.3, f32[768]{0:T(1024)S(1)} %subtract_add_fusion), kind=kOutput, calls=%fused_computation.26 | convolution fusion | flops 1817395200 | bytes 2958336 | tf_op jit(solution)/shard_map/dot_general | solution.py:112
  126.5 162.6 %all-gather.8.cloned.1.call-done = bf16[768,14232]{1,0:T(8,128)(2,1)} async-done(((bf16[24,14232]{1,0:T(8,128)(2,1)}), bf16[768,14232]{1,0:T(8,128)(2,1)}) %all-gather.8.cloned.1.call-update) | async-done | bytes 21860368 | tf_op jit(solution)/shard_map/all_gather | solution.py:91
  289.1 17.9 %fusion.2 = bf16[192,14232]{1,0:T(8,128)(2,1)} fusion(bf16[192,768]{1,0:T(8,128)(2,1)S(1)} %fusion.14, bf16[768,14232]{1,0:T(8,128)(2,1)} %all-gather.8.cloned.1.call-done, bf16[192,14232]{1,0:T(8,128)(2,1)} %param.5, f32[192]{0:T(256)S(1)} %get-tuple-element.12, f32[192]{0:T(256)S(1)} %subtract_add_fusion.1), kind=kOutput, calls=%fused_computation.6 | convolution fusion | flops 4210850304 | bytes 33086976 | tf_op jit(solution)/shard_map/dot_general | solution.py:89
  (15 shorter events, 0.1 us)
Async XLA Ops:
  7.2 3.5 %copy-start = (s32[6144]{0:T(1024)S(1)}, s32[6144]{0:T(1024)}, u32[]{:S(2)}) copy-start(s32[6144]{0:T(1024)} %param.7) | copy-start | bytes 73732
  7.2 79.3 %all-gather.4.cloned.1.call-start = ((), (), s32[]{:S(2)}) async-start(), calls=%async_computation | async-start | bytes 1216512 | tf_op jit(solution)/shard_map/all_gather | solution.py:86
  10.6 109.6 %all-gather.6.cloned.1.call-start = ((), (), s32[]{:S(2)}) async-start(), calls=%async_computation.1 | async-start | bytes 2654208 | tf_op jit(solution)/shard_map/all_gather | solution.py:107
  15.1 71.4 %copy-start.2 = (bf16[192,768]{1,0:T(8,128)(2,1)S(1)}, bf16[192,768]{1,0:T(8,128)(2,1)}, u32[]{:S(2)}) copy-start(bf16[192,768]{1,0:T(8,128)(2,1)} %param.4) | copy-start | bytes 884740
  88.9 31.2 %copy-start.1 = (bf16[192,768]{1,0:T(8,128)(2,1)S(1)}, bf16[192,768]{1,0:T(8,128)(2,1)}, u32[]{:S(2)}) copy-start(bf16[192,768]{1,0:T(8,128)(2,1)} %fusion.13) | copy-start | bytes 884740
  88.9 200.2 %all-gather.8.cloned.1.call-start = ((), (), s32[]{:S(2)}) async-start(), calls=%async_computation.2 | async-start | bytes 22708224 | tf_op jit(solution)/shard_map/all_gather | solution.py:91
Sparse Core Ops, SparseCore 0:
  11.1 75.2 all-gather.3
  89.0 31.0 all-gather.5
  123.3 165.8 all-gather.7
where the time goes:
time: 314 us
  waiting for transfers between devices  254 us (81%)
  matrix products  33.7 us (11%)
  between operations  13.9 us (4%)
  local copies, waits for them, and re-layouts  8.95 us (3%)
    all_gather x1, waiting for transfers between devices, shards(): lax.all_gather(send_rest, 'row', axis=0, tiled=True)  163 us
    all_gather x1, waiting for transfers between devices, shards(): lax.all_gather(send_window, 'row', axis=0, tiled=True)  65.7 us
    all_gather x1, waiting for transfers between devices, shards(): piece = lax.all_gather(mixed_window, 'col', axis=1, tiled=True)  25.4 us
    dot_general x1, matrix products, shards(): jnp.dot(placement, lax.all_gather(send_rest, 'row', axis=0, tiled=True),...  17.9 us
    dot_general x1, matrix products, shards(): gathered = jnp.dot(piece, picker, preferred_element_type=jnp.float32)  6.39 us
  transfers between devices with their start and end apart: 3, of which 3 were waited for; matrix products, arithmetic and copies ran while one was open for 7% of the time, Pallas kernels for 0%

commit v1 on v0

--- a/solution.py
+++ b/solution.py
@@ -104,7 +104,20 @@
     column_retained, column_selected, column_provider = item_weight_values(
         column_identifiers, lasting_node, vanishing_node, retained_pair, selected_pair
     )
-    piece = lax.all_gather(mixed_window, "col", axis=1, tiled=True)
+    ways, here, step = (lax.axis_size("col"), lax.axis_index("col"), mixed_window.shape[1])
+    shape = [n * ways if d == 1 else n for d, n in enumerate(mixed_window.shape)]
+    piece = lax.dynamic_update_slice_in_dim(
+        jnp.zeros(shape, mixed_window.dtype), mixed_window, here * step, axis=1
+    )
+    going_up = going_down = mixed_window
+    for far in range(1, ways // 2 + 1):
+        going_up = lax.ppermute(going_up, "col", [(d, (d + 1) % ways) for d in range(ways)])
+        piece = lax.dynamic_update_slice_in_dim(piece, going_up, (here - far) % ways * step, axis=1)
+        if 2 * far < ways:
+            going_down = lax.ppermute(going_down, "col", [(d, (d - 1) % ways) for d in range(ways)])
+            piece = lax.dynamic_update_slice_in_dim(
+                piece, going_down, (here + far) % ways * step, axis=1
+            )
     piece_width = piece.shape[1]
     picker = (jnp.arange(piece_width, dtype=jnp.int32)[:, None] == column_provider[None, :]).astype(
         jnp.bfloat16

time: 314 us -> 282 us (0.90)
  waiting for transfers between devices: 254 us -> 206 us
  starting transfers between devices: 0.3 us -> 15.4 us
  local copies, waits for them, and re-layouts: 8.95 us -> 13.3 us
  matrix products: 33.7 us -> 29.4 us
    all_gather x1, waiting for transfers between devices: 163 us -> 135 us  [shards(): lax.all_gather(send_rest, 'row', axis=0, tiled=True)]
    all_gather x1 -> x0, waiting for transfers between devices: 25.4 us -> none  [shards(): piece = lax.all_gather(mixed_window, 'col', axis=1, tiled=True)]
    ppermute x0 -> x7, starting transfers between devices: none -> 15.4 us  [the longest x4 13.8 us: shards(): lax.ppermute(going_up, 'col', [(d, (d + 1) % ways) for d in range(ways)])]
    ppermute x0 -> x7, waiting for transfers between devices: none -> 9.62 us  [the longest x4 7.49 us: shards(): lax.ppermute(going_up, 'col', [(d, (d + 1) % ways) for d in range(ways)])]
    all_gather x1, waiting for transfers between devices: 65.7 us -> 61.4 us  [shards(): lax.all_gather(send_window, 'row', axis=0, tiled=True)]
  transfers between devices with their start and end apart: 3 -> 9, of which waited for: 3 -> 6; matrix products, arithmetic and copies ran while one was open for 7% -> 9% of each run, Pallas kernels for 0% -> 0%
where the time goes in v1:
time: 282 us
  waiting for transfers between devices  206 us (73%)
  matrix products  29.4 us (10%)
  starting transfers between devices  15.4 us (5%)
  between operations  14.4 us (5%)
  local copies, waits for them, and re-layouts  13.3 us (5%)
  other arithmetic  2.9 us (1%)
    all_gather x1, waiting for transfers between devices, shards(): lax.all_gather(send_rest, 'row', axis=0, tiled=True)  135 us
    all_gather x1, waiting for transfers between devices, shards(): lax.all_gather(send_window, 'row', axis=0, tiled=True)  61.4 us
    dot_general x1, matrix products, shards(): jnp.dot(placement, lax.all_gather(send_rest, 'row', axis=0, tiled=True),...  17.2 us
    ppermute x4, starting transfers between devices, shards(): lax.ppermute(going_up, 'col', [(d, (d + 1) % ways) for d in range(ways)])  13.8 us
    ppermute x4, waiting for transfers between devices, shards(): lax.ppermute(going_up, 'col', [(d, (d + 1) % ways) for d in range(ways)])  7.49 us
  transfers between devices with their start and end apart: 9, of which 6 were waited for; matrix products, arithmetic and copies ran while one was open for 9% of the time, Pallas kernels for 0%

profile of v1, /device:TPU:1, one launch (start us, length us, event | category | flops | bytes accessed | tf_op | source)
XLA Modules:
  0.0 281.9 jit_solution(4324352239070329332)
XLA Ops:
  7.2 0.8 fusion.32
  8.7 1.8 convolution_convert_fusion.1
  10.6 4.3 %convolution_convert_fusion = bf16[24,14232]{1,0:T(8,128)(2,1)} fusion(bf16[24,192]{1,0:T(8,128)(2,1)S(1)} %convolution_convert_fusion.2, bf16[192,14232]{1,0:T(8,128)(2,1)} %param.5), kind=kOutput, calls=%fused_computation.7 | convolution fusion | flops 131503680 | bytes 6157440 | tf_op jit(solution)/shard_map/dot_general | solution.py:72
  14.9 4.5 %gather_fusion = s32[768]{0:T(1024)S(1)} fusion(s32[6144]{0:T(1024)S(1)} %copy-done, s32[1024]{0:T(1024)S(1)} %get-tuple-element.27), kind=kCustom, calls=%fused_computation | custom fusion | bytes 9216 | tf_op jit(solution)/shard_map/gather | solution.py:10
  19.4 4.5 %gather_fusion.1 = s32[768]{0:T(1024)S(1)} fusion(s32[6144]{0:T(1024)S(1)} %copy-done, s32[1024]{0:T(1024)S(1)} %get-tuple-element.26), kind=kCustom, calls=%fused_computation.1 | custom fusion | bytes 9216 | tf_op jit(solution)/shard_map/gather | solution.py:11
  24.3 0.8 fusion.14
  25.0 61.4 %all-gather.3.cloned.1.call-done = bf16[768,768]{1,0:T(8,128)(2,1)} async-done(((bf16[24,768]{1,0:T(8,128)(2,1)}), bf16[768,768]{1,0:T(8,128)(2,1)}) %all-gather.3.cloned.1.call-update) | async-done | bytes 1179664 | tf_op jit(solution)/shard_map/all_gather | solution.py:86
  86.7 1.0 copy-done.2
  88.2 6.8 %collective-permute-start = (bf16[192,768]{1,0:T(8,128)(2,1)S(1)}, bf16[192,768]{1,0:T(8,128)(2,1)}, u32[]{:S(2)}, u32[]{:S(2)}) collective-permute-start(bf16[192,768]{1,0:T(8,128)(2,1)S(1)} %get-tuple-element.25), channel_id=1, source_target_pairs={{0,1},{1,2},{2,3},{3,4},{4,5},{5,6},{6,7},{7,0},{8,9},{9,10},{10,1... | collective-permute-start | bytes 884744 | tf_op jit(solution)/shard_map/ppermute | solution.py:114
  95.0 0.9 convert_reduce_fusion.1
  95.9 2.7 collective-permute-done
  98.6 2.6 collective-permute-start.2
  101.9 3.3 %collective-permute-done.2 = bf16[192,768]{1,0:T(8,128)(2,1)} collective-permute-done((bf16[192,768]{1,0:T(8,128)(2,1)}, bf16[192,768]{1,0:T(8,128)(2,1)}, u32[]{:S(2)}, u32[]{:S(2)}) %collective-permute-start.2) | collective-permute-done | bytes 294944 | tf_op jit(solution)/shard_map/ppermute | solution.py:114
  105.2 2.5 collective-permute-start.4
  107.7 1.0 constant_dynamic-update-slice_fusion.6
  108.7 1.0 constant_dynamic-update-slice_fusion.5
  109.7 1.4 collective-permute-start.5
  111.1 1.0 constant_dynamic-update-slice_fusion.4
  112.1 2.0 collective-permute-start.6
  114.1 2.1 collective-permute-done.5
  116.3 1.4 collective-permute-done.6
  117.7 4.7 %fusion.12 = bf16[192,768]{1,0:T(8,128)(2,1)} fusion(bf16[192,6144]{1,0:T(8,128)(2,1)S(1)} %constant_dynamic-update-slice_fusion, s32[768]{0:T(1024)S(1)} %fusion.6, bf16[192,768]{1,0:T(8,128)(2,1)S(1)} %get-tuple-element.25, f32[768]{0:T(1024)S(1)} %get-tuple-element.3, f32[768]{0:T(1024)S(1)} %subtract_add_fusion), kind=kOutput, calls=%fused_computation.26 | convolution fusion | flops 1817395200 | bytes 2958336 | tf_op jit(solution)/shard_map/dot_general | solution.py:125
  122.4 135.4 %all-gather.5.cloned.1.call-done = bf16[768,14232]{1,0:T(8,128)(2,1)} async-done(((bf16[24,14232]{1,0:T(8,128)(2,1)}), bf16[768,14232]{1,0:T(8,128)(2,1)}) %all-gather.5.cloned.1.call-update) | async-done | bytes 21860368 | tf_op jit(solution)/shard_map/all_gather | solution.py:91
  257.8 17.2 %fusion.2 = bf16[192,14232]{1,0:T(8,128)(2,1)} fusion(bf16[192,768]{1,0:T(8,128)(2,1)S(1)} %fusion.14, bf16[768,14232]{1,0:T(8,128)(2,1)} %all-gather.5.cloned.1.call-done, bf16[192,14232]{1,0:T(8,128)(2,1)} %param.5, f32[192]{0:T(256)S(1)} %get-tuple-element.12, f32[192]{0:T(256)S(1)} %subtract_add_fusion.1), kind=kOutput, calls=%fused_computation.6 | convolution fusion | flops 4210850304 | bytes 33086976 | tf_op jit(solution)/shard_map/dot_general | solution.py:89
  (34 shorter events, 2.5 us)
Async XLA Ops:
  7.2 7.7 %copy-start = (s32[6144]{0:T(1024)S(1)}, s32[6144]{0:T(1024)}, u32[]{:S(2)}) copy-start(s32[6144]{0:T(1024)} %param.7) | copy-start | bytes 73732
  7.2 79.3 %all-gather.3.cloned.1.call-start = ((), (), s32[]{:S(2)}) async-start(), calls=%async_computation | async-start | bytes 1216512 | tf_op jit(solution)/shard_map/all_gather | solution.py:86
  10.6 247.3 %all-gather.5.cloned.1.call-start = ((), (), s32[]{:S(2)}) async-start(), calls=%async_computation.1 | async-start | bytes 22708224 | tf_op jit(solution)/shard_map/all_gather | solution.py:91
  23.8 62.9 %copy-start.1 = (bf16[192,768]{1,0:T(8,128)(2,1)S(1)}, bf16[192,768]{1,0:T(8,128)(2,1)}, u32[]{:S(2)}) copy-start(bf16[192,768]{1,0:T(8,128)(2,1)} %param.4) | copy-start | bytes 884740
  86.5 1.3 copy-start.2
  88.2 10.5 %collective-permute-start = (bf16[192,768]{1,0:T(8,128)(2,1)S(1)}, bf16[192,768]{1,0:T(8,128)(2,1)}, u32[]{:S(2)}, u32[]{:S(2)}) collective-permute-start(bf16[192,768]{1,0:T(8,128)(2,1)S(1)} %get-tuple-element.25), channel_id=1, source_target_pairs={{0,1},{1,2},{2,3},{3,4},{4,5},{5,6},{6,7},{7,0},{8,9},{9,10},{10,1... | collective-permute-start | bytes 884744 | tf_op jit(solution)/shard_map/ppermute | solution.py:114
  95.0 6.3 %collective-permute-start.1 = (bf16[192,768]{1,0:T(8,128)(2,1)S(1)}, bf16[192,768]{1,0:T(8,128)(2,1)}, u32[]{:S(2)}, u32[]{:S(2)}) collective-permute-start(bf16[192,768]{1,0:T(8,128)(2,1)S(1)} %get-tuple-element.25), channel_id=1, source_target_pairs={{0,7},{1,0},{2,1},{3,2},{4,3},{5,4},{6,5},{7,6},{8,15},{9,8},{10,9... | collective-permute-start | bytes 884744 | tf_op jit(solution)/shard_map/ppermute | solution.py:117
  98.6 6.6 %collective-permute-start.2 = (bf16[192,768]{1,0:T(8,128)(2,1)}, bf16[192,768]{1,0:T(8,128)(2,1)}, u32[]{:S(2)}, u32[]{:S(2)}) collective-permute-start(bf16[192,768]{1,0:T(8,128)(2,1)} %collective-permute-done), channel_id=1, source_target_pairs={{0,1},{1,2},{2,3},{3,4},{4,5},{5,6},{6,7},{7,0},{8,9},{9,10},{10,1... | collective-permute-start | bytes 884744 | tf_op jit(solution)/shard_map/ppermute | solution.py:114
  101.2 8.5 %collective-permute-start.3 = (bf16[192,768]{1,0:T(8,128)(2,1)}, bf16[192,768]{1,0:T(8,128)(2,1)S(1)}, u32[]{:S(2)}, u32[]{:S(2)}) collective-permute-start(bf16[192,768]{1,0:T(8,128)(2,1)} %collective-permute-done.1), channel_id=1, source_target_pairs={{0,7},{1,0},{2,1},{3,2},{4,3},{5,4},{6,5},{7,6},{8,15},{9,8},{10,9... | collective-permute-start | bytes 884744 | tf_op jit(solution)/shard_map/ppermute | solution.py:117
  105.2 6.9 %collective-permute-start.4 = (bf16[192,768]{1,0:T(8,128)(2,1)}, bf16[192,768]{1,0:T(8,128)(2,1)S(1)}, u32[]{:S(2)}, u32[]{:S(2)}) collective-permute-start(bf16[192,768]{1,0:T(8,128)(2,1)} %collective-permute-done.2), channel_id=1, source_target_pairs={{0,1},{1,2},{2,3},{3,4},{4,5},{5,6},{6,7},{7,0},{8,9},{9,10},{10,1... | collective-permute-start | bytes 884744 | tf_op jit(solution)/shard_map/ppermute | solution.py:114
  109.7 6.6 %collective-permute-start.5 = (bf16[192,768]{1,0:T(8,128)(2,1)S(1)}, bf16[192,768]{1,0:T(8,128)(2,1)S(1)}, u32[]{:S(2)}, u32[]{:S(2)}) collective-permute-start(bf16[192,768]{1,0:T(8,128)(2,1)S(1)} %collective-permute-done.3), channel_id=1, source_target_pairs={{0,7},{1,0},{2,1},{3,2},{4,3},{5,4},{6,5},{7,6},{8,15},{9,8},{10,9... | collective-permute-start | bytes 884744 | tf_op jit(solution)/shard_map/ppermute | solution.py:117
  112.1 5.6 %collective-permute-start.6 = (bf16[192,768]{1,0:T(8,128)(2,1)S(1)}, bf16[192,768]{1,0:T(8,128)(2,1)S(1)}, u32[]{:S(2)}, u32[]{:S(2)}) collective-permute-start(bf16[192,768]{1,0:T(8,128)(2,1)S(1)} %collective-permute-done.4), channel_id=1, source_target_pairs={{0,1},{1,2},{2,3},{3,4},{4,5},{5,6},{6,7},{7,0},{8,9},{9,10},{10,1... | collective-permute-start | bytes 884744 | tf_op jit(solution)/shard_map/ppermute | solution.py:114
Sparse Core Ops, SparseCore 0:
  11.1 75.2 all-gather.2
  89.6 168.1 all-gather.4
